TPU v7x, 32 devices: a whole 2x2x4 slice. The times are simulated.
32 devices in a mesh: pole: 2 (over y), row: 8 (over z, x), col: 2 (over core).
Axes of the slice: x: 2, y: 2, z: 4, core: 2. Of those that a mesh axis runs over, the one named last changes fastest.
Arguments:
- known_inverse: float32 [16, 128, 1024], P('pole', 'col', 'row'), parts along dimension 0, may hold values from -1 to 3, as said below
- first_factor: float32 [2048, 512], P(('pole', 'row')), parts along dimension 0, may hold values from -0.5 to 0.5
- first_corner: float32 [1024, 512], P('pole'), parts along dimension 0, may hold values from -1 to 5, as said below
- first_ancestors: int32 [1024], P('pole'), parts along dimension 0, may hold values from 0 to 1023, as said below
- second_factor: float32 [2048, 512], P(('pole', 'row')), parts along dimension 0, may hold values from -0.75 to 0.75
- second_link: float32 [1024, 512], P('pole'), parts along dimension 0, may hold values from -0.25 to 0.25
- second_corner: float32 [1024, 512], P('pole', 'col'), parts along dimension 0, may hold values from -1 to 5, as said below
- second_ancestors: int32 [512], P('pole'), parts along dimension 0, may hold values from 0 to 1023, as said below
Outputs:
- first_column: float32 [2048, 512], P(('pole', 'row'), 'col'), parts along dimension 0
- first_diagonal: float32 [1024, 512], P('pole', 'col'), parts along dimension 0
- second_column: float32 [2048, 512], P(('pole', 'row'), 'col'), parts along dimension 0
- second_cross: float32 [1024, 512], P('pole', 'col'), parts along dimension 0
- second_diagonal: float32 [1024, 512], P('pole', 'col'), parts along dimension 0
There are 2 independent parts, one for each index of `pole`. A program takes and returns all parts, laid end to end along the dimension named above; each array names one. Nothing has to cross between parts.
Inputs may be any that keep to these rules, and one draw needn't show every extreme that they name: `known_inverse`: K is symmetric. `first_corner`: symmetric. `second_corner`: symmetric. `first_ancestors`: distinct row numbers; every block of 128 consecutive row numbers starting at a multiple of 128 holds at least one of them. `second_ancestors`: distinct row numbers, each of which is also in first_ancestors; every block of 128 consecutive row numbers starting at a multiple of 128 holds at least one of them.
All inputs are finite; a program needn't handle non-finite values.
Results may differ from a plain program's by a relative error of at most 0.000084.
Values sent between devices are 32-bit elements; how exact they have to be, the bound alone decides.
A program may use at most 128 MiB of HBM per device.

v0:
```python
import jax
import jax.numpy as jnp
from jax import lax
from jax.sharding import PartitionSpec as P

HIGH = lax.Precision.HIGHEST


def product(left, right):
    return jnp.dot(left, right, precision=HIGH, preferred_element_type=jnp.float32)


def transposed_product(left, right):
    return lax.dot_general(
        left, right, (((0,), (0,)), ((), ())), precision=HIGH, preferred_element_type=jnp.float32
    )


def local_mask(ancestors, row_start, block_rows):
    global_rows = row_start + jnp.arange(block_rows, dtype=jnp.int32)
    return jnp.any(ancestors[:, None] == global_rows[None, :], axis=0).astype(jnp.float32)[:, None]


def on_device(
    known_inverse,
    first_factor,
    first_corner,
    first_ancestors,
    second_factor,
    second_link,
    second_corner,
    second_ancestors,
):
    groups, share_rows, block_rows = known_inverse.shape
    half_width = second_corner.shape[1]
    col_index = lax.axis_index("col")
    row_start = lax.axis_index("row") * block_rows
    first_mask = local_mask(first_ancestors, row_start, block_rows)
    second_mask = local_mask(second_ancestors, row_start, block_rows)
    first_masked = first_factor * first_mask
    second_masked = second_factor * second_mask
    share_start = col_index * share_rows
    first_piece = lax.dynamic_slice_in_dim(first_masked, share_start, share_rows, 0)
    second_piece = lax.dynamic_slice_in_dim(second_masked, share_start, share_rows, 0)
    columns = known_inverse.reshape(groups * share_rows, block_rows)

    def add_piece(piece):
        return transposed_product(columns, piece)

    first_partial = add_piece(lax.all_gather(first_piece, "row", axis=0, tiled=True))
    second_partial = add_piece(lax.all_gather(second_piece, "row", axis=0, tiled=True))
    first_image = lax.psum_scatter(first_partial, "col", scatter_dimension=1, tiled=True)
    first_column = -(first_image * first_mask)
    first_full = lax.all_gather(first_column, "col", axis=1, tiled=True)
    diagonal_partial = transposed_product(first_masked, first_column)
    corner_half = lax.dynamic_slice_in_dim(first_corner, col_index * half_width, half_width, 1)
    first_diagonal = corner_half - lax.psum(diagonal_partial, "row")
    diagonal_full = lax.all_gather(first_diagonal, "col", axis=1, tiled=True)
    second_image = lax.psum_scatter(second_partial, "col", scatter_dimension=1, tiled=True)
    link_half = lax.dynamic_slice_in_dim(second_link, col_index * half_width, half_width, 1)
    second_column = -((second_image + product(first_full, link_half)) * second_mask)
    second_half = lax.dynamic_slice_in_dim(second_masked, col_index * half_width, half_width, 1)
    cross_partial = transposed_product(first_full, second_half)
    closing_partial = transposed_product(second_masked, second_column)
    cross_total, closing_total = lax.psum((cross_partial, closing_partial), "row")
    second_cross = -(cross_total + product(diagonal_full, link_half))
    second_diagonal = second_corner - closing_total - transposed_product(second_link, second_cross)
    return (first_column, first_diagonal, second_column, second_cross, second_diagonal)


def solution(mesh):
    return jax.shard_map(
        on_device,
        mesh=mesh,
        in_specs=(
            P("pole", "col", "row"),
            P(("pole", "row"), None),
            P("pole", None),
            P("pole"),
            P(("pole", "row"), None),
            P("pole", None),
            P("pole", "col"),
            P("pole"),
        ),
        out_specs=(
            P(("pole", "row"), "col"),
            P("pole", "col"),
            P(("pole", "row"), "col"),
            P("pole", "col"),
            P("pole", "col"),
        ),
        check_vma=False,
    )
```

profile of v0, /device:TPU:1, one launch (start us, length us, event | category | flops | bytes accessed | tf_op | source)
XLA Modules:
  0.0 233.0 jit_solution(5799603692559722448)
XLA Ops:
  7.2 0.0 copy-start
  7.2 0.0 all-gather.4.cloned.1.call-start
  7.2 0.0 copy-start.8
  7.3 0.7 copy-done.8
  8.0 0.1 compare_reduce_fusion
  8.2 1.0 broadcast_multiply_fusion.1
  9.2 0.0 copy-start.6
  9.2 0.7 constant_dynamic-slice_fusion.1
  9.9 0.0 copy-start.9
  9.9 0.0 all-gather.4.cloned.1.call-update
  9.9 0.0 all-gather.6.cloned.1.call-start
  10.0 0.6 copy-done.9
  10.6 0.1 compare_reduce_fusion.1
  10.7 0.0 copy-done.6
  10.7 0.1 broadcast_multiply_fusion
  10.8 0.0 copy-start.2
  10.8 0.7 constant_dynamic-slice_fusion
  11.5 0.0 all-gather.6.cloned.1.call-update
  11.5 0.0 reduce-scatter.3.cloned.1.call-start
  11.5 39.8 %all-gather.4.cloned.1.call-done = f32[512,512]{1,0:T(8,128)} async-done(((f32[64,512]{1,0:T(8,128)}), f32[512,512]{1,0:T(8,128)}) %all-gather.4.cloned.1.call-update) | async-done | bytes 1048592 | tf_op jit(solution)/shard_map/all_gather | solution.py:50
  51.4 0.0 copy-done.2
  51.4 3.7 %convolution_bitcast_fusion.2 = f32[128,512]{0,1:T(8,128)} fusion(f32[512,512]{1,0:T(8,128)} %all-gather.4.cloned.1.call-done, f32[512,128]{1,0:T(8,128)S(1)} %bitcast.22), kind=kOutput, calls=%fused_computation.5 | convolution fusion | flops 402653184 | bytes 1572864 | tf_op jit(solution)/shard_map/dot_general | solution.py:14
  55.1 0.0 reduce-scatter.3.cloned.1.call-update
  55.1 0.0 reduce-scatter.5.cloned.1.call-start
  55.2 37.9 %all-gather.6.cloned.1.call-done = f32[512,512]{1,0:T(8,128)} async-done(((f32[64,512]{1,0:T(8,128)}), f32[512,512]{1,0:T(8,128)}) %all-gather.6.cloned.1.call-update) | async-done | bytes 1048592 | tf_op jit(solution)/shard_map/all_gather | solution.py:51
  93.1 3.7 %convolution_bitcast_fusion.1 = f32[128,512]{0,1:T(8,128)} fusion(f32[512,512]{1,0:T(8,128)} %all-gather.6.cloned.1.call-done, f32[512,128]{1,0:T(8,128)S(1)} %bitcast.23), kind=kOutput, calls=%fused_computation.4 | convolution fusion | flops 402653184 | bytes 1572864 | tf_op jit(solution)/shard_map/dot_general | solution.py:14
  96.8 0.0 reduce-scatter.5.cloned.1.call-update
  96.8 0.0 all-reduce.3.cloned.1.call-start
  96.9 7.5 %reduce-scatter.3.cloned.1.call-done = f32[128,256]{0,1:T(8,128)} async-done(((f32[128,512]{0,1:T(8,128)}), f32[128,256]{0,1:T(8,128)}) %reduce-scatter.3.cloned.1.call-update) | async-done | bytes 131088 | tf_op jit(solution)/shard_map/reduce_scatter | solution.py:52
  104.4 0.9 multiply_negate_fusion
  105.3 2.0 all_gather.14
  107.3 1.4 fusion.6
  108.7 1.4 fusion.11
  110.1 5.9 %reduce-scatter.5.cloned.1.call-done = f32[128,256]{0,1:T(8,128)} async-done(((f32[128,512]{0,1:T(8,128)}), f32[128,256]{0,1:T(8,128)}) %reduce-scatter.5.cloned.1.call-update) | async-done | bytes 131088 | tf_op jit(solution)/shard_map/reduce_scatter | solution.py:59
  116.0 0.0 copy-done
  116.0 1.9 fusion.3
  117.9 0.0 copy-start.7
  117.9 1.4 fusion.12
  119.3 0.0 all-reduce.3.cloned.1.call-update
  119.3 0.0 all-gather.8.cloned.1.call-start
  119.4 91.3 %all-reduce.3.cloned.1.call-done = (f32[512,256]{1,0:T(8,128)}, f32[512,256]{1,0:T(8,128)}, f32[512,256]{1,0:T(8,128)}) async-done(((f32[512,256]{1,0:T(8,128)}, f32[512,256]{1,0:T(8,128)}, f32[512,256]{1,0:T(8,128)}), (f32[512,256]{1,0:T(8,128)}, f32[512,256]{1,0:T(8,128)}, f32[512,256]{1,0:T(8,128)})) %all-reduce.3.cloned.1.call-update) | async-done | bytes 1572880 | tf_op jit(solution)/shard_map/psum | solution.py:57
  210.6 0.0 copy-done.7
  210.6 1.9 dynamic-slice_subtract_fusion
  212.6 0.0 copy-start.5
  212.6 0.0 all-gather.8.cloned.1.call-update
  212.6 0.8 copy.19
  213.4 0.8 copy.20
  214.1 7.1 %all-gather.8.cloned.1.call-done = f32[512,512]{1,0:T(8,128)} async-done(((f32[512,256]{1,0:T(8,128)}), f32[512,512]{1,0:T(8,128)}) %all-gather.8.cloned.1.call-update) | async-done | bytes 1048592 | tf_op jit(solution)/shard_map/all_gather | solution.py:58
  221.2 0.0 copy-done.5
  221.2 0.0 copy-start.3
  221.2 0.0 copy-start.4
  221.2 2.3 fusion
  223.5 0.0 copy-start.1
  223.5 0.0 copy-done.3
  223.5 0.0 copy-done.4
  223.5 2.6 %fusion.1 = f32[512,256]{1,0:T(8,128)} fusion(f32[512,256]{1,0:T(8,128)S(1)} %fusion, f32[512,512]{1,0:T(8,128)S(1)} %copy-done, f32[512,256]{1,0:T(8,128)S(1)} %copy-done.3, f32[512,256]{1,0:T(8,128)S(1)} %copy-done.4), kind=kOutput, calls=%fused_computation.3 | convolution fusion | flops 805568512 | bytes 3145728 | tf_op jit(solution)/shard_map/dot_general | solution.py:14
  226.2 0.0 copy-done.1
  (3 shorter events, 0.0 us)
Async XLA Ops:
  7.2 108.8 %copy-start = (f32[512,512]{1,0:T(8,128)S(1)}, f32[512,512]{1,0:T(8,128)}, u32[]{:S(2)}) copy-start(f32[512,512]{1,0:T(8,128)} %param.13) | copy-start | bytes 3145732
  7.2 44.2 %all-gather.4.cloned.1.call-start = ((), (), s32[]{:S(2)}) async-start(), calls=%async_computation.2 | async-start | bytes 1179648 | tf_op jit(solution)/shard_map/all_gather | solution.py:50
  7.2 0.8 copy-start.8
  9.2 1.5 copy-start.6
  9.9 0.7 copy-start.9
  9.9 83.2 %all-gather.6.cloned.1.call-start = ((), (), s32[]{:S(2)}) async-start(), calls=%async_computation.4 | async-start | bytes 1179648 | tf_op jit(solution)/shard_map/all_gather | solution.py:51
  10.8 40.6 %copy-start.2 = (f32[8,64,128]{2,1,0:T(8,128)S(1)}, f32[8,64,128]{2,1,0:T(8,128)}, u32[]{:S(2)}) copy-start(f32[8,64,128]{2,1,0:T(8,128)} %param.8) | copy-start | bytes 786436
  11.5 92.9 %reduce-scatter.3.cloned.1.call-start = ((), (), s32[]{:S(2)}) async-start(), calls=%async_computation.3 | async-start | bytes 393216 | tf_op jit(solution)/shard_map/reduce_scatter | solution.py:52
  55.1 60.8 %reduce-scatter.5.cloned.1.call-start = ((), (), s32[]{:S(2)}) async-start(), calls=%async_computation.5 | async-start | bytes 393216 | tf_op jit(solution)/shard_map/reduce_scatter | solution.py:59
  96.8 113.8 %all-reduce.3.cloned.1.call-start = ((), (), s32[]{:S(2)}) async-start(), calls=%async_computation.7 | async-start | bytes 3145728 | tf_op jit(solution)/shard_map/psum | solution.py:57
  117.9 92.8 %copy-start.7 = (f32[512,512]{1,0:T(8,128)S(1)}, f32[512,512]{1,0:T(8,128)}, u32[]{:S(2)}) copy-start(f32[512,512]{1,0:T(8,128)} %param.10) | copy-start | bytes 3145732
  119.3 101.9 %all-gather.8.cloned.1.call-start = ((), (), s32[]{:S(2)}) async-start(), calls=%async_computation.6 | async-start | bytes 1572864 | tf_op jit(solution)/shard_map/all_gather | solution.py:58
  212.6 8.6 %copy-start.5 = (f32[512,256]{1,0:T(8,128)S(1)}, f32[512,256]{1,0:T(8,128)}, u32[]{:S(2)}) copy-start(f32[512,256]{1,0:T(8,128)} %get-tuple-element.16) | copy-start | bytes 1572868
  221.2 2.3 copy-start.3
  221.2 2.3 copy-start.4
  223.5 2.7 %copy-start.1 = (f32[512,256]{1,0:T(8,128)}, f32[512,256]{1,0:T(8,128)S(1)}, u32[]{:S(2)}) copy-start(f32[512,256]{1,0:T(8,128)S(1)} %fusion) | copy-start | bytes 1572868
Sparse Core Ops, SparseCore 0:
  10.7 40.6 all-gather.3
  54.1 38.9 all-gather.5
  95.9 8.4 reduce-scatter.2
  107.1 8.8 reduce-scatter.4
  120.2 90.3 all-reduce.2
  212.7 8.4 all-gather.7
where the time goes:
time: 234 us; the launch traced here: 233 us
  waiting for transfers between devices  190 us (81%)
  matrix products  18.5 us (8%)
  between operations  14.2 us (6%)
  other arithmetic  4.26 us (2%)
  local copies, waits for them, and re-layouts  4.25 us (2%)
    psum x1, waiting for transfers between devices, on_device(): first_diagonal = corner_half - lax.psum(diagonal_partial, 'row')  91.3 us
    all_gather x1, waiting for transfers between devices, on_device(): lax.all_gather(first_piece, 'row', axis=0, tiled=True)  39.8 us
    all_gather x1, waiting for transfers between devices, on_device(): lax.all_gather(second_piece, 'row', axis=0, tiled=True)  37.9 us
    dot_general x6, matrix products, transposed_product(): lax.dot_general(left, right, (((0,), (0,)), ((), ())), precision=HIGH, pr...  14.3 us
    reduce_scatter x1, waiting for transfers between devices, on_device(): lax.psum_scatter(first_partial, 'col', scatter_dimension=1, tiled=True)  7.53 us
    all_gather x1, waiting for transfers between devices, on_device(): diagonal_full = lax.all_gather(first_diagonal, 'col', axis=1, tiled=True)  7.07 us
    reduce_scatter x1, waiting for transfers between devices, on_device(): lax.psum_scatter(second_partial, 'col', scatter_dimension=1, tiled=True)  5.86 us
  transfers between devices with their start and end apart: 6, of which 6 were waited for; matrix products, arithmetic and copies ran while one was open for 6% of the time, Pallas kernels for 0%

commit v1 on v0

--- a/solution.py
+++ b/solution.py
@@ -1,9 +1,16 @@
+import functools
+
 import jax
 import jax.numpy as jnp
 from jax import lax
+from jax.experimental import pallas as pl
+from jax.experimental.pallas import tpu as pltpu
 from jax.sharding import PartitionSpec as P
 
 HIGH = lax.Precision.HIGHEST
+MESH = pl.DeviceIdType.MESH
+LANES_OF_RING = 2
+VMEM_FOR_WHOLE = 40 * 2**20
 
 
 def product(left, right):
@@ -21,7 +28,7 @@
     return jnp.any(ancestors[:, None] == global_rows[None, :], axis=0).astype(jnp.float32)[:, None]
 
 
-def on_device(
+def on_device_collectives(
     known_inverse,
     first_factor,
     first_corner,
@@ -68,7 +75,316 @@
     return (first_column, first_diagonal, second_column, second_cross, second_diagonal)
 
 
+def split(value):
+    high = value.astype(jnp.bfloat16)
+    return high, (value - high.astype(jnp.float32)).astype(jnp.bfloat16)
+
+
+def dot(left, right):
+    return jnp.dot(left, right, preferred_element_type=jnp.float32)
+
+
+def dot3(left, right):
+    (left_high, left_low), (right_high, right_low) = left, right
+    return dot(left_high, right_high) + (dot(left_low, right_high) + dot(left_high, right_low))
+
+
+def ring_kernel(
+    n,
+    known,
+    factor_one,
+    corner_one,
+    ancestors_one,
+    factor_two,
+    link,
+    corner_two,
+    ancestors_two,
+    column_one,
+    diagonal_one,
+    column_two,
+    cross_two,
+    diagonal_two,
+    k_raw,
+    f_raw,
+    f_high,
+    f_low,
+    t_buf,
+    own,
+    link_buf,
+    corner_buf,
+    link_half,
+    corner_half,
+    corner_two_buf,
+    link_split,
+    half_split,
+    local_sem,
+    ring_send,
+    ring_recv,
+    pair_send,
+    pair_recv,
+):
+    half = n // 2
+    blocks = half + 1
+    share = k_raw.shape[3]
+    block = 2 * share
+    width = link_buf.shape[0]
+    hw = width // 2
+    me_row = lax.axis_index("row")
+    me_col = lax.axis_index("col")
+    other_col = 1 - me_col
+
+    length = n // LANES_OF_RING
+
+    def row_at(position):
+        position = lax.rem(position + n, n)
+        lane = position // length
+        step = position + lane * (2 * length - 1 - 2 * position)
+        return step * LANES_OF_RING + lane
+
+    lane = lax.rem(me_row, LANES_OF_RING)
+    step = me_row // LANES_OF_RING
+    place = step + lane * (2 * length - 1 - 2 * step)
+    targets = (row_at(place + 1), row_at(place - 1))
+
+    barrier = pltpu.get_barrier_semaphore()
+    for target in targets:
+        pl.semaphore_signal(barrier, inc=1, device_id={"row": target}, device_id_type=MESH)
+    pl.semaphore_signal(barrier, inc=1, device_id={"col": other_col}, device_id_type=MESH)
+
+    count = [0]
+
+    def local(src, dst):
+        copy = pltpu.make_async_copy(src, dst, local_sem.at[count[0]])
+        count[0] += 1
+        copy.start()
+        return copy
+
+    f_one = [local(factor_one.at[pl.ds(h * share, share)], f_raw.at[0, h, 0]) for h in range(2)]
+    f_two = [local(factor_two.at[pl.ds(h * share, share)], f_raw.at[0, h, 1]) for h in range(2)]
+    k_own = [local(known.at[row_at(place + i)], k_raw.at[0, me_col, i]) for i in range(blocks)]
+    my_columns = pl.ds(pl.multiple_of(me_col * hw, 128), hw)
+    rest = [
+        local(link, link_buf),
+        local(corner_one, corner_buf),
+        local(link.at[:, my_columns], link_half),
+        local(corner_one.at[:, my_columns], corner_half),
+        local(corner_two, corner_two_buf),
+    ]
+
+    def slot(direction, t):
+        return 0 if t == 0 else n - 1 if t == half else 2 * t - 1 + direction
+
+    offsets = [0] * n
+    for t in range(1, half):
+        offsets[slot(0, t)], offsets[slot(1, t)] = -t, t
+    offsets[n - 1] = half
+    cut = half // 2
+
+    def view(piece, at, which):
+        if piece < 2:
+            return f_raw.at[at, which, piece]
+        if piece == 2:
+            return k_raw.at[at, which]
+        if piece == 3:
+            return k_raw.at[at, which, pl.ds(0, cut)]
+        return k_raw.at[at, which, pl.ds(cut, blocks - cut)]
+
+    def pieces(direction, t):
+        if t < half:
+            return (0, 1, 2)
+        return (0, 3) if direction == 0 else (1, 4)
+
+    def ring(direction, t, piece):
+        return pltpu.make_async_remote_copy(
+            src_ref=view(piece, slot(direction, t - 1), me_col),
+            dst_ref=view(piece, slot(direction, t), me_col),
+            send_sem=ring_send.at[direction, t - 1, piece],
+            recv_sem=ring_recv.at[direction, t - 1, piece],
+            device_id={"row": targets[direction]},
+            device_id_type=MESH,
+        )
+
+    def pair(at, piece, which):
+        return pltpu.make_async_remote_copy(
+            src_ref=view(piece, at, which),
+            dst_ref=view(piece, at, which),
+            send_sem=pair_send.at[at, piece],
+            recv_sem=pair_recv.at[at, piece],
+            device_id={"col": other_col},
+            device_id_type=MESH,
+        )
+
+    sent = []
+
+    def go(copy):
+        copy.start()
+        sent.append(copy)
+
+    pl.semaphore_wait(barrier, 3)
+    for piece, waits in ((0, f_one), (1, f_two), (2, k_own)):
+        for copy in waits:
+            copy.wait()
+        for direction in range(2):
+            go(ring(direction, 1, piece))
+    go(pair(0, 2, me_col))
+
+    for copy in rest:
+        copy.wait()
+    link_split[0], link_split[1] = split(link_buf[...])
+    half_split[0], half_split[1] = split(link_half[...])
+    corner_link = dot3(split(corner_buf[...]), (half_split[0], half_split[1]))
+    cross_two[...] = -corner_link
+    diagonal_one[...] = corner_half[...]
+    diagonal_two[...] = corner_two_buf[...] + dot3(split(link_buf[...].T), split(corner_link))
+    own[...] = jnp.zeros_like(own)
+
+    def mask_of(ancestors, row_start):
+        rows = row_start + lax.broadcasted_iota(jnp.int32, (block, ancestors.shape[1]), 0)
+        same = jnp.where(rows == ancestors[...], 1.0, 0.0)
+        return jnp.max(same, axis=1, keepdims=True)
+
+    def k_block(a, b):
+        i = (offsets[a] - offsets[b]) % n
+        if i <= half:
+            return k_raw[b, :, i].reshape(block, block)
+        return k_raw[a, :, n - i].reshape(block, block).T
+
+    def mine(ref, start):
+        return ref[:, pl.ds(pl.multiple_of(start + me_col * hw, 128), hw)]
+
+    def process(k):
+        row_start = row_at(place + offsets[k]) * block
+        first = f_raw[k, :, 0].reshape(block, width) * mask_of(ancestors_one, row_start)
+        second = f_raw[k, :, 1].reshape(block, width) * mask_of(ancestors_two, row_start)
+        reduced = second - dot3(split(first), (link_split[0], link_split[1]))
+        rows = pl.ds(k * block, block)
+        both = jnp.concatenate([first, reduced], axis=1)
+        f_high[rows, :], f_low[rows, :] = split(both)
+        my_high = jnp.concatenate([mine(f_high.at[rows], 0), mine(f_high.at[rows], width)], axis=1)
+        my_low = jnp.concatenate([mine(f_low.at[rows], 0), mine(f_low.at[rows], width)], axis=1)
+        own[...] += dot3(split(k_block(0, k)), (my_high, my_low))
+        diagonal_part = dot3(split(k_block(k, k)), (my_high, my_low))
+        if k == 0:
+            left = both.T
+            right_high, right_low = split(diagonal_part)
+        else:
+            past = pl.ds(0, k * block)
+            line_high, line_low = split(jnp.concatenate([k_block(k, j) for j in range(k)], axis=1))
+            image = dot3((line_high, line_low), (f_high[past, :], f_low[past, :]))
+            t_buf[...] = image
+            left = jnp.concatenate([both.T, image.T], axis=1)
+            image_mine = jnp.concatenate([mine(t_buf, 0), mine(t_buf, width)], axis=1)
+            image_high, image_low = split(image_mine + diagonal_part)
+            right_high = jnp.concatenate([image_high, my_high], axis=0)
+            right_low = jnp.concatenate([image_low, my_low], axis=0)
+        left_high, left_low = split(left)
+        add = dot3((left_high[:width], left_low[:width]), (right_high, right_low))
+        diagonal_one[...] += add[:, :hw]
+        cross_two[...] += add[:, hw:]
+        diagonal_two[...] += dot3((left_high[width:], left_low[width:]), (right_high[:, hw:], right_low[:, hw:]))
+
+    pair(0, 2, other_col).wait_recv()
+    process(0)
+    for t in range(1, half):
+        for piece in range(3):
+            for direction in range(2):
+                ring(direction, t, piece).wait_recv()
+                for later in pieces(direction, t + 1):
+                    if later == piece or (piece == 2 and later > 2):
+                        go(ring(direction, t + 1, later))
+                go(pair(slot(direction, t), piece, me_col))
+        for direction in range(2):
+            for piece in range(3):
+                pair(slot(direction, t), piece, other_col).wait_recv()
+            process(slot(direction, t))
+    last = [(direction, pieces(direction, half)[i]) for i in range(2) for direction in range(2)]
+    for direction, piece in last:
+        ring(direction, half, piece).wait_recv()
+        go(pair(n - 1, piece, me_col))
+    for direction, piece in last:
+        pair(n - 1, piece, other_col).wait_recv()
+    process(n - 1)
+    first_rows = mask_of(ancestors_one, me_row * block)
+    second_rows = mask_of(ancestors_two, me_row * block)
+    column_one[...] = -(own[:, :hw] * first_rows)
+    column_two[...] = -(own[:, hw:] * second_rows)
+    for copy in sent:
+        copy.wait_send()
+
+
+def on_device_ring(
+    n,
+    known_inverse,
+    first_factor,
+    first_corner,
+    first_ancestors,
+    second_factor,
+    second_link,
+    second_corner,
+    second_ancestors,
+):
+    groups, share, block = known_inverse.shape
+    width = second_link.shape[0]
+    hw = second_corner.shape[1]
+    f32, bf16 = jnp.float32, jnp.bfloat16
+    blocks = n // 2 + 1
+    anywhere = pl.BlockSpec(memory_space=pl.ANY)
+    vmem = pl.BlockSpec(memory_space=pltpu.VMEM)
+    square = jax.ShapeDtypeStruct((width, hw), f32)
+    column = jax.ShapeDtypeStruct((block, hw), f32)
+    return pl.pallas_call(
+        functools.partial(ring_kernel, n),
+        out_shape=(column, square, column, square, square),
+        in_specs=[anywhere, anywhere, anywhere, vmem, anywhere, anywhere, anywhere, vmem],
+        out_specs=(vmem,) * 5,
+        scratch_shapes=[
+            pltpu.VMEM((n, 2, blocks, share, block), f32),
+            pltpu.VMEM((n, 2, 2, share, width), f32),
+            pltpu.VMEM((n * block, 2 * width), bf16),
+            pltpu.VMEM((n * block, 2 * width), bf16),
+            pltpu.VMEM((block, 2 * width), f32),
+            pltpu.VMEM((block, width), f32),
+            pltpu.VMEM((width, width), f32),
+            pltpu.VMEM((width, width), f32),
+            pltpu.VMEM((width, hw), f32),
+            pltpu.VMEM((width, hw), f32),
+            pltpu.VMEM((width, hw), f32),
+            pltpu.VMEM((2, width, width), bf16),
+            pltpu.VMEM((2, width, hw), bf16),
+            pltpu.SemaphoreType.DMA((9 + blocks,)),
+            pltpu.SemaphoreType.DMA((2, n // 2, 5)),
+            pltpu.SemaphoreType.DMA((2, n // 2, 5)),
+            pltpu.SemaphoreType.DMA((n, 5)),
+            pltpu.SemaphoreType.DMA((n, 5)),
+        ],
+        compiler_params=pltpu.CompilerParams(collective_id=0, has_side_effects=True),
+    )(
+        known_inverse,
+        first_factor,
+        first_corner,
+        first_ancestors.reshape(1, -1),
+        second_factor,
+        second_link,
+        second_corner,
+        second_ancestors.reshape(1, -1),
+    )
+
+
 def solution(mesh):
+    def on_device(*args):
+        n = mesh.shape["row"]
+        groups, share, block = args[0].shape
+        width = args[5].shape[0]
+        held = 4 * n * block * (n * block + 4 * width)
+        fits = (
+            mesh.shape["col"] == 2
+            and n % 4 == 0
+            and groups == n
+            and block == 2 * share
+            and held <= VMEM_FOR_WHOLE
+        )
+        return on_device_ring(n, *args) if fits else on_device_collectives(*args)
+
     return jax.shard_map(
         on_device,
         mesh=mesh,

time: 234 us -> 53.9 us (0.23)
  waiting for transfers between devices: 190 us -> 0 us
  Pallas kernels: 0 us -> 46.9 us
  matrix products: 18.5 us -> 0 us
  between operations: 14.2 us -> 0.65 us
  other arithmetic: 4.26 us -> 0 us
    psum x1 -> x0, waiting for transfers between devices: 91.3 us -> none  [on_device(): first_diagonal = corner_half - lax.psum(diagonal_partial, 'row')]
    all_gather x3 -> x0, waiting for transfers between devices: 84.8 us -> none  [the longest x1 39.8 us: on_device(): lax.all_gather(first_piece, 'row', axis=0, tiled=True)]
    pallas_call x0 -> x1, Pallas kernels: none -> 46.9 us  [on_device_ring(): pl.pallas_call(functools.partial(ring_kernel, n), out_shape=(column, squa...]
    dot_general x8 -> x0, matrix products: 18.5 us -> none  [the longest x6 14.3 us: transposed_product(): lax.dot_general(left, right, (((0,), (0,)), ((), ())), precision=HIGH, pr...]
    reduce_scatter x2 -> x0, waiting for transfers between devices: 13.4 us -> none  [the longest x1 7.53 us: on_device(): lax.psum_scatter(first_partial, 'col', scatter_dimension=1, tiled=True)]
    unnamed x22 -> x11, local copies, waits for them, and re-layouts: 2.9 us -> 6.19 us
  transfers between devices with their start and end apart: 6 -> 0, of which waited for: 6 -> 0; matrix products, arithmetic and copies ran while one was open for 6% -> 0% of each run, Pallas kernels for 0% -> 0%
where the time goes in v1:
time: 53.9 us; the launch traced here: 53.7 us
  Pallas kernels  46.9 us (87%)
  local copies, waits for them, and re-layouts  6.19 us (11%)
  between operations  0.65 us (1%)
    pallas_call x1, Pallas kernels, on_device_ring(): pl.pallas_call(functools.partial(ring_kernel, n), out_shape=(column, squa...  46.9 us
    unnamed x11, local copies, waits for them, and re-layouts  6.19 us

profile of v1, /device:TPU:1, one launch (start us, length us, event | category | flops | bytes accessed | tf_op | source)
XLA Modules:
  0.0 53.7 jit_solution(3000032836352144493)
XLA Ops:
  0.6 46.9 %shard_map.119 = (f32[128,256]{1,0:T(8,128)}, f32[512,256]{1,0:T(8,128)}, f32[128,256]{1,0:T(8,128)}, f32[512,256]{1,0:T(8,128)}, f32[512,256]{1,0:T(8,128)}) custom-call(f32[8,64,128]{2,1,0:T(8,128)} %known.1, f32[128,512]{1,0:T(8,128)} %factor_one.1, f32[512,512]{1,0:T(8,128)} %corner_one.1, s32[1,512]{1,0:T(1,128)} %bitcast.2, f32[128,512]{1,0:T(8,128)} %factor_two.1, ...), custom_call_target="tpu_custom_call" | custom-call | tf_op jit(solution)/shard_map/pallas_call | solution.py:335
  47.5 1.6 %copy.18 = f32[128,256]{1,0:T(8,128)} copy(f32[128,256]{1,0:T(8,128)} %get-tuple-element.10) | data formatting | bytes 262144
  49.1 0.0 copy-start.2
  49.1 0.0 copy-start.1
  49.1 1.9 %copy.19 = f32[512,256]{1,0:T(8,128)} copy(f32[512,256]{1,0:T(8,128)} %get-tuple-element.11) | data formatting | bytes 1048576
  51.0 0.0 copy-done.2
  51.0 0.7 %copy.20 = f32[128,256]{1,0:T(8,128)} copy(f32[128,256]{1,0:T(8,128)S(1)} %copy-done.2) | data formatting | bytes 262144
  51.7 0.0 copy-done.1
  51.7 0.0 copy-start
  51.7 0.8 %copy.21 = f32[512,256]{1,0:T(8,128)} copy(f32[512,256]{1,0:T(8,128)S(1)} %copy-done.1) | data formatting | bytes 1048576
  52.5 0.4 copy-done
  52.9 0.8 %copy.22 = f32[512,256]{1,0:T(8,128)} copy(f32[512,256]{1,0:T(8,128)S(1)} %copy-done) | data formatting | bytes 1048576
Async XLA Ops:
  49.1 1.9 %copy-start.2 = (f32[128,256]{1,0:T(8,128)S(1)}, f32[128,256]{1,0:T(8,128)}, u32[]{:S(2)}) copy-start(f32[128,256]{1,0:T(8,128)} %get-tuple-element.12) | copy-start | bytes 393220
  49.1 2.6 %copy-start.1 = (f32[512,256]{1,0:T(8,128)S(1)}, f32[512,256]{1,0:T(8,128)}, u32[]{:S(2)}) copy-start(f32[512,256]{1,0:T(8,128)} %get-tuple-element.13) | copy-start | bytes 1572868
  51.7 1.2 %copy-start = (f32[512,256]{1,0:T(8,128)S(1)}, f32[512,256]{1,0:T(8,128)}, u32[]{:S(2)}) copy-start(f32[512,256]{1,0:T(8,128)} %get-tuple-element.14) | copy-start | bytes 1572868

commit v2 on v1

--- a/solution.py
+++ b/solution.py
@@ -117,6 +117,7 @@
     corner_two_buf,
     link_split,
     half_split,
+    left,
     local_sem,
     ring_send,
     ring_recv,
@@ -178,26 +179,24 @@
     for t in range(1, half):
         offsets[slot(0, t)], offsets[slot(1, t)] = -t, t
     offsets[n - 1] = half
-    cut = half // 2
-
-    def view(piece, at, which):
+
+    def held(at):
+        return blocks if offsets[at] <= 0 else half
+
+    def view(piece, at, which, amount):
         if piece < 2:
             return f_raw.at[at, which, piece]
-        if piece == 2:
-            return k_raw.at[at, which]
-        if piece == 3:
-            return k_raw.at[at, which, pl.ds(0, cut)]
-        return k_raw.at[at, which, pl.ds(cut, blocks - cut)]
+        return k_raw.at[at, which, pl.ds(0, amount)]
 
     def pieces(direction, t):
         if t < half:
             return (0, 1, 2)
-        return (0, 3) if direction == 0 else (1, 4)
+        return (0,) if direction == 0 else (1, 2)
 
     def ring(direction, t, piece):
         return pltpu.make_async_remote_copy(
-            src_ref=view(piece, slot(direction, t - 1), me_col),
-            dst_ref=view(piece, slot(direction, t), me_col),
+            src_ref=view(piece, slot(direction, t - 1), me_col, held(slot(direction, t))),
+            dst_ref=view(piece, slot(direction, t), me_col, held(slot(direction, t))),
             send_sem=ring_send.at[direction, t - 1, piece],
             recv_sem=ring_recv.at[direction, t - 1, piece],
             device_id={"row": targets[direction]},
@@ -206,8 +205,8 @@
 
     def pair(at, piece, which):
         return pltpu.make_async_remote_copy(
-            src_ref=view(piece, at, which),
-            dst_ref=view(piece, at, which),
+            src_ref=view(piece, at, which, held(at)),
+            dst_ref=view(piece, at, which, held(at)),
             send_sem=pair_send.at[at, piece],
             recv_sem=pair_recv.at[at, piece],
             device_id={"col": other_col},
@@ -245,14 +244,17 @@
 
     def k_block(a, b):
         i = (offsets[a] - offsets[b]) % n
-        if i <= half:
+        if i < half or (i == half and held(b) == blocks):
             return k_raw[b, :, i].reshape(block, block)
         return k_raw[a, :, n - i].reshape(block, block).T
 
     def mine(ref, start):
         return ref[:, pl.ds(pl.multiple_of(start + me_col * hw, 128), hw)]
 
-    def process(k):
+    def mine_of(ref, rows):
+        return jnp.concatenate([mine(ref.at[rows], 0), mine(ref.at[rows], width)], axis=1)
+
+    def prepare(k):
         row_start = row_at(place + offsets[k]) * block
         first = f_raw[k, :, 0].reshape(block, width) * mask_of(ancestors_one, row_start)
         second = f_raw[k, :, 1].reshape(block, width) * mask_of(ancestors_two, row_start)
@@ -260,56 +262,97 @@
         rows = pl.ds(k * block, block)
         both = jnp.concatenate([first, reduced], axis=1)
         f_high[rows, :], f_low[rows, :] = split(both)
-        my_high = jnp.concatenate([mine(f_high.at[rows], 0), mine(f_high.at[rows], width)], axis=1)
-        my_low = jnp.concatenate([mine(f_low.at[rows], 0), mine(f_low.at[rows], width)], axis=1)
+        left[k % 2, 0, :, :block], left[k % 2, 1, :, :block] = split(both.T)
+
+    def image_of(k, slots):
+        if not slots:
+            return jnp.zeros((block, 2 * width), jnp.float32)
+        total = None
+        line_high, line_low = split(jnp.concatenate([k_block(k, j) for j in slots], axis=1))
+        at, start = 0, 0
+        while at < len(slots):
+            upto = at
+            while upto + 1 < len(slots) and slots[upto + 1] == slots[upto] + 1:
+                upto += 1
+            past = pl.ds(slots[at] * block, (upto + 1 - at) * block)
+            columns = slice(at * block, (upto + 1) * block)
+            term = dot3((line_high[:, columns], line_low[:, columns]), (f_high[past, :], f_low[past, :]))
+            total = term if total is None else total + term
+            at = upto + 1
+        return total
+
+    def finish(k, image):
+        rows = pl.ds(k * block, block)
+        my_high, my_low = mine_of(f_high, rows), mine_of(f_low, rows)
         own[...] += dot3(split(k_block(0, k)), (my_high, my_low))
         diagonal_part = dot3(split(k_block(k, k)), (my_high, my_low))
         if k == 0:
-            left = both.T
+            depth = block
             right_high, right_low = split(diagonal_part)
         else:
-            past = pl.ds(0, k * block)
-            line_high, line_low = split(jnp.concatenate([k_block(k, j) for j in range(k)], axis=1))
-            image = dot3((line_high, line_low), (f_high[past, :], f_low[past, :]))
+            depth = 2 * block
             t_buf[...] = image
-            left = jnp.concatenate([both.T, image.T], axis=1)
+            left[k % 2, 0, :, block:], left[k % 2, 1, :, block:] = split(image.T)
             image_mine = jnp.concatenate([mine(t_buf, 0), mine(t_buf, width)], axis=1)
             image_high, image_low = split(image_mine + diagonal_part)
             right_high = jnp.concatenate([image_high, my_high], axis=0)
             right_low = jnp.concatenate([image_low, my_low], axis=0)
-        left_high, left_low = split(left)
-        add = dot3((left_high[:width], left_low[:width]), (right_high, right_low))
+        add = dot3((left[k % 2, 0, :width, :depth], left[k % 2, 1, :width, :depth]), (right_high, right_low))
         diagonal_one[...] += add[:, :hw]
         cross_two[...] += add[:, hw:]
-        diagonal_two[...] += dot3((left_high[width:], left_low[width:]), (right_high[:, hw:], right_low[:, hw:]))
-
-    pair(0, 2, other_col).wait_recv()
-    process(0)
-    for t in range(1, half):
-        for piece in range(3):
-            for direction in range(2):
-                ring(direction, t, piece).wait_recv()
-                for later in pieces(direction, t + 1):
-                    if later == piece or (piece == 2 and later > 2):
-                        go(ring(direction, t + 1, later))
-                go(pair(slot(direction, t), piece, me_col))
+        diagonal_two[...] += dot3(
+            (left[k % 2, 0, width:, :depth], left[k % 2, 1, width:, :depth]),
+            (right_high[:, hw:], right_low[:, hw:]),
+        )
+
+    def early(k, before):
+        gaps = {j: (offsets[k] - offsets[j]) % n for j in range(before)}
+        return [j for j, gap in gaps.items() if gap < half or (gap == half and held(j) == blocks)]
+
+    def take(direction, t, piece):
+        ring(direction, t, piece).wait_recv()
+        if piece in pieces(direction, t + 1) and t < half:
+            go(ring(direction, t + 1, piece))
+        go(pair(slot(direction, t), piece, me_col))
+
+    def take_both(t, piece):
         for direction in range(2):
-            for piece in range(3):
-                pair(slot(direction, t), piece, other_col).wait_recv()
-            process(slot(direction, t))
-    last = [(direction, pieces(direction, half)[i]) for i in range(2) for direction in range(2)]
-    for direction, piece in last:
-        ring(direction, half, piece).wait_recv()
-        go(pair(n - 1, piece, me_col))
-    for direction, piece in last:
-        pair(n - 1, piece, other_col).wait_recv()
-    process(n - 1)
+            if piece in pieces(direction, t):
+                take(direction, t, piece)
+
+    def paired(at, which_pieces):
+        for piece in which_pieces:
+            pair(at, piece, other_col).wait_recv()
+
+    paired(0, (2,))
+    prepare(0)
+    finish(0, None)
+    for t in range(1, half + 1):
+        slots = sorted({slot(0, t), slot(1, t)})
+        known = min(slots)
+        take_both(t, 0)
+        take_both(t, 1)
+        images = {}
+        for k in slots:
+            paired(k, (0, 1))
+            prepare(k)
+            images[k] = image_of(k, early(k, known))
+        take_both(t, 2)
+        for k in slots:
+            paired(k, (2,))
+            rest_of = [j for j in range(k) if j not in early(k, known)]
+            finish(k, images[k] + image_of(k, rest_of))
     first_rows = mask_of(ancestors_one, me_row * block)
     second_rows = mask_of(ancestors_two, me_row * block)
     column_one[...] = -(own[:, :hw] * first_rows)
     column_two[...] = -(own[:, hw:] * second_rows)
     for copy in sent:
         copy.wait_send()
+
+
+def place_kernel(*refs):
+    for source, target in zip(refs[:5], refs[5:]):
+        target[...] = source[...]
 
 
 def on_device_ring(
@@ -332,7 +375,7 @@
     vmem = pl.BlockSpec(memory_space=pltpu.VMEM)
     square = jax.ShapeDtypeStruct((width, hw), f32)
     column = jax.ShapeDtypeStruct((block, hw), f32)
-    return pl.pallas_call(
+    results = pl.pallas_call(
         functools.partial(ring_kernel, n),
         out_shape=(column, square, column, square, square),
         in_specs=[anywhere, anywhere, anywhere, vmem, anywhere, anywhere, anywhere, vmem],
@@ -351,11 +394,12 @@
             pltpu.VMEM((width, hw), f32),
             pltpu.VMEM((2, width, width), bf16),
             pltpu.VMEM((2, width, hw), bf16),
+            pltpu.VMEM((2, 2, 2 * width, 2 * block), bf16),
             pltpu.SemaphoreType.DMA((9 + blocks,)),
-            pltpu.SemaphoreType.DMA((2, n // 2, 5)),
-            pltpu.SemaphoreType.DMA((2, n // 2, 5)),
-            pltpu.SemaphoreType.DMA((n, 5)),
-            pltpu.SemaphoreType.DMA((n, 5)),
+            pltpu.SemaphoreType.DMA((2, n // 2, 3)),
+            pltpu.SemaphoreType.DMA((2, n // 2, 3)),
+            pltpu.SemaphoreType.DMA((n, 3)),
+            pltpu.SemaphoreType.DMA((n, 3)),
         ],
         compiler_params=pltpu.CompilerParams(collective_id=0, has_side_effects=True),
     )(
@@ -368,6 +412,12 @@
         second_corner,
         second_ancestors.reshape(1, -1),
     )
+    return pl.pallas_call(
+        place_kernel,
+        out_shape=(column, square, column, square, square),
+        in_specs=[vmem] * 5,
+        out_specs=(vmem,) * 5,
+    )(*results)
 
 
 def solution(mesh):

time: 53.9 us -> 51.3 us (0.952)
  local copies, waits for them, and re-layouts: 6.19 us -> 0 us
  Pallas kernels: 46.9 us -> 50.4 us
    unnamed x11 -> x0, local copies, waits for them, and re-layouts: 6.19 us -> none
    pallas_call x0 -> x1, Pallas kernels: none -> 2.7 us  [on_device_ring(): pl.pallas_call(place_kernel, out_shape=(column, square, column, square, s...]
    pallas_call x1, Pallas kernels: 46.9 us -> 47.7 us  [on_device_ring(): pl.pallas_call(functools.partial(ring_kernel, n), out_shape=(column, squa...]
where the time goes in v2:
time: 51.3 us; the launch traced here: 51.1 us
  Pallas kernels  50.4 us (98%)
  between operations  0.64 us (1%)
    pallas_call x1, Pallas kernels, on_device_ring(): pl.pallas_call(functools.partial(ring_kernel, n), out_shape=(column, squa...  47.7 us
    pallas_call x1, Pallas kernels, on_device_ring(): pl.pallas_call(place_kernel, out_shape=(column, square, column, square, s...  2.7 us

profile of v2, /device:TPU:1, one launch (start us, length us, event | category | flops | bytes accessed | tf_op | source)
XLA Modules:
  0.0 51.1 jit_solution(8493160969394692016)
XLA Ops:
  0.6 47.7 %shard_map.119 = (f32[128,256]{1,0:T(8,128)}, f32[512,256]{1,0:T(8,128)}, f32[128,256]{1,0:T(8,128)}, f32[512,256]{1,0:T(8,128)}, f32[512,256]{1,0:T(8,128)}) custom-call(f32[8,64,128]{2,1,0:T(8,128)} %known.1, f32[128,512]{1,0:T(8,128)} %factor_one.1, f32[512,512]{1,0:T(8,128)} %corner_one.1, s32[1,512]{1,0:T(1,128)} %bitcast.2, f32[128,512]{1,0:T(8,128)} %factor_two.1, ...), custom_call_target="tpu_custom_call" | custom-call | tf_op jit(solution)/shard_map/pallas_call | solution.py:378
  48.4 2.7 %shard_map.120 = (f32[128,256]{1,0:T(8,128)}, f32[512,256]{1,0:T(8,128)}, f32[128,256]{1,0:T(8,128)}, f32[512,256]{1,0:T(8,128)}, f32[512,256]{1,0:T(8,128)}) custom-call(f32[128,256]{1,0:T(8,128)} %get-tuple-element.10.refs_0_, f32[512,256]{1,0:T(8,128)} %get-tuple-element.11.refs_1_, f32[128,256]{1,0:T(8,128)} %get-tuple-element.12.refs_2_, ...), custom_call_target="tpu_custom_call" | custom-call | tf_op jit(solution)/shard_map/pallas_call | solution.py:415
